TPU v7x, 32 devices: a whole 2x2x4 slice. The times are simulated.
32 devices in a mesh: slab: 16 (over z, x, core), grp: 2 (over y).
Axes of the slice: x: 2, y: 2, z: 4, core: 2. Of those that a mesh axis runs over, the one named last changes fastest.
Arguments:
- capture: float32 [2, 262144], P(None, ('slab', 'grp')), may hold values from -6 to 6
- dropped: int32 [16], P('slab'), may hold values from 0 to 8191
Outputs:
- max_held: float32 [128, 128, 128], P('slab', 'grp')
- coherent: float32 [2, 128, 128, 128], P(None, 'slab', 'grp')
All inputs are finite; a program needn't handle non-finite values.
Results may differ from a plain program's by a relative error of at most 0.0001.
Values sent between devices are 32-bit elements; how exact they have to be, the bound alone decides.
A program may use at most 128 MiB of HBM per device.

v0:
```python
import math

import jax
import jax.numpy as jnp
from jax import lax
from jax.sharding import PartitionSpec as P

NCH = 256
HOP = 64
KW = 128
LW = 128
Q = 128
BLOCKS = 2


def passed_along(array, axis, by):
    length = lax.axis_size(axis)
    pairs = [(i, i + by) for i in range(length) if 0 <= i + by < length]
    return lax.ppermute(array, axis, pairs)


def matmul_exact(left_side, right_side):
    return jnp.dot(
        left_side, right_side, precision=lax.Precision.HIGHEST, preferred_element_type=jnp.float32
    )


def channelize(extended, hop_count, channels, stamp, first_hop):
    lead_hops = NCH // HOP - 1
    tap_index = jnp.arange(NCH, dtype=jnp.int32)
    window = 0.5 - 0.5 * jnp.cos(2.0 * math.pi * tap_index.astype(jnp.float32) / NCH)
    scaling = 1.0 / jnp.sqrt(jnp.sum(window * window))
    tap_turns = (tap_index[:, None] * channels[None, :] % NCH).astype(jnp.float32) * (
        2.0 * math.pi / NCH
    )
    cos_table = (window * scaling)[:, None] * jnp.cos(tap_turns)
    sin_table = (window * scaling)[:, None] * jnp.sin(tap_turns)
    hop_rows = extended.reshape(2, hop_count + lead_hops, HOP)
    real_sum = jnp.zeros((hop_count, channels.shape[0]), jnp.float32)
    imag_sum = jnp.zeros((hop_count, channels.shape[0]), jnp.float32)
    for lag_index in range(lead_hops + 1):
        real_rows = hop_rows[0, lag_index : lag_index + hop_count]
        imag_rows = hop_rows[1, lag_index : lag_index + hop_count]
        cos_rows = cos_table[lag_index * HOP : (lag_index + 1) * HOP]
        sin_rows = sin_table[lag_index * HOP : (lag_index + 1) * HOP]
        real_sum = real_sum + matmul_exact(real_rows, cos_rows) + matmul_exact(imag_rows, sin_rows)
        imag_sum = imag_sum + matmul_exact(imag_rows, cos_rows) - matmul_exact(real_rows, sin_rows)
    hop_numbers = first_hop + jnp.arange(hop_count, dtype=jnp.int32)
    clock_mod = (stamp % NCH + hop_numbers * HOP) % NCH
    chan_turns = (clock_mod[:, None] * channels[None, :] % NCH).astype(jnp.float32) * (
        2.0 * math.pi / NCH
    )
    cosine = jnp.cos(chan_turns)
    sine = jnp.sin(chan_turns)
    return jnp.stack([real_sum * cosine + imag_sum * sine, imag_sum * cosine - real_sum * sine])


def on_device(capture, dropped):
    slab_count = lax.axis_size("slab")
    group_count = lax.axis_size("grp")
    slab_index = lax.axis_index("slab")
    group_index = lax.axis_index("grp")
    lead_hops = NCH // HOP - 1
    local_samples = capture.shape[1]
    margin = passed_along(capture[:, local_samples - lead_hops * HOP :], ("slab", "grp"), 1)
    every_drop = lax.all_gather(dropped, "slab", axis=0, tiled=True)
    positions = jnp.arange(every_drop.shape[0], dtype=jnp.int32)
    through = jnp.sum(jnp.where(positions <= slab_index, every_drop, 0))
    stamp = slab_index * (BLOCKS * Q * HOP) + through
    own_width = KW // group_count
    extended = jnp.concatenate([margin, capture], axis=1)
    local_hops = local_samples // HOP
    channels = jnp.arange(KW + LW, dtype=jnp.int32)
    shifted = channelize(extended, local_hops, channels, stamp, group_index * local_hops)
    lower_bank = lax.all_to_all(shifted[:, :, :KW], "grp", split_axis=2, concat_axis=1, tiled=True)
    upper_bank = lax.all_gather(shifted[:, :, KW:], "grp", axis=1, tiled=True)
    freq_bins = jnp.arange(Q, dtype=jnp.int32)
    dft_turns = (freq_bins[:, None] * freq_bins[None, :] % Q).astype(jnp.float32) * (
        2.0 * math.pi / Q
    )
    dft_cos = jnp.cos(dft_turns) / math.sqrt(Q)
    dft_sin = jnp.sin(dft_turns) / math.sqrt(Q)
    largest = jnp.zeros((Q, own_width * LW), jnp.float32)
    real_total = jnp.zeros((Q, own_width * LW), jnp.float32)
    imag_total = jnp.zeros((Q, own_width * LW), jnp.float32)
    for block_index in range(BLOCKS):
        lower_real = lower_bank[0, block_index * Q : (block_index + 1) * Q]
        lower_imag = lower_bank[1, block_index * Q : (block_index + 1) * Q]
        upper_real = upper_bank[0, block_index * Q : (block_index + 1) * Q]
        upper_imag = upper_bank[1, block_index * Q : (block_index + 1) * Q]
        prod_real = (
            lower_real[:, :, None] * upper_real[:, None, :]
            + lower_imag[:, :, None] * upper_imag[:, None, :]
        ).reshape(Q, own_width * LW)
        prod_imag = (
            lower_imag[:, :, None] * upper_real[:, None, :]
            - lower_real[:, :, None] * upper_imag[:, None, :]
        ).reshape(Q, own_width * LW)
        surf_real = matmul_exact(dft_cos, prod_real) + matmul_exact(dft_sin, prod_imag)
        surf_imag = matmul_exact(dft_cos, prod_imag) - matmul_exact(dft_sin, prod_real)
        largest = jnp.maximum(largest, jnp.sqrt(surf_real * surf_real + surf_imag * surf_imag))
        real_total = real_total + surf_real
        imag_total = imag_total + surf_imag
    clock_period = Q * HOP
    cycle_turns = (freq_bins * (stamp % clock_period) % clock_period).astype(jnp.float32) * (
        2.0 * math.pi / clock_period
    )
    cycle_cos = jnp.cos(cycle_turns)[:, None]
    cycle_sin = jnp.sin(cycle_turns)[:, None]
    norm_scale = 1.0 / math.sqrt(slab_count * BLOCKS)
    aligned_real = ((real_total * cycle_cos + imag_total * cycle_sin) * norm_scale).reshape(
        Q, own_width, LW
    )
    aligned_imag = ((imag_total * cycle_cos - real_total * cycle_sin) * norm_scale).reshape(
        Q, own_width, LW
    )
    largest = largest.reshape(Q, own_width, LW)
    coherent = lax.psum_scatter(
        jnp.stack([aligned_real, aligned_imag]), "slab", scatter_dimension=1, tiled=True
    )
    every_held = lax.pmax(largest, "slab")
    own_bins = Q // slab_count
    max_held = lax.dynamic_slice_in_dim(every_held, slab_index * own_bins, own_bins, 0)
    return (max_held, coherent)


def solution(mesh):
    in_specs = (P(None, ("slab", "grp")), P("slab"))
    out_specs = (P("slab", "grp", None), P(None, "slab", "grp", None))
    return jax.shard_map(
        on_device, mesh=mesh, in_specs=in_specs, out_specs=out_specs, check_vma=False
    )
```

profile of v0, /device:TPU:0, one launch (start us, length us, event | category | flops | bytes accessed | tf_op | source)
XLA Modules:
  0.0 346.0 jit_solution(9556243154251408101)
XLA Ops:
  7.2 0.8 slice.81
  7.9 4.9 %collective-permute-start = (f32[2,192]{1,0:T(2,128)S(1)}, f32[2,192]{1,0:T(2,128)S(1)}, u32[]{:S(2)}, u32[]{:S(2)}) collective-permute-start(f32[2,192]{1,0:T(2,128)S(1)} %slice.81), channel_id=1, source_target_pairs={{0,1},{1,2},{2,3},{3,4},{4,5},{5,6},{6,7},{7,8},{8,9},{9,10},{10,1... | collective-permute-start | bytes 4616 | tf_op jit(solution)/shard_map/ppermute | solution.py:19
  12.8 0.6 multiply_reduce_fusion
  14.1 1.2 dynamic-slice
  15.4 0.8 dynamic-update-slice
  16.1 12.3 %all-reduce = s32[16]{0:T(128)S(1)} all-reduce(s32[16]{0:T(128)S(1)} %dynamic-update-slice), channel_id=1, replica_groups=mesh['slab'=16,'grp'=2] {'slab'}, use_global_device_ids=true, to_apply=%add | all-reduce | flops 16 | bytes 128
  28.4 0.6 fusion.76
  30.5 1.1 sine_multiply_fusion
  31.6 1.0 pad_maximum_fusion.2
  32.7 0.3 fusion.42
  33.2 0.2 convolution_subtract_fusion.5
  33.5 0.3 convolution_add_fusion.4
  33.7 0.3 convolution_subtract_fusion.4
  34.0 0.3 convolution_add_fusion.3
  34.3 0.3 convolution_subtract_fusion.3
  34.5 0.3 convolution_add_fusion.2
  34.8 0.2 convolution_add_fusion.11
  35.0 0.3 convolution_add_fusion.10
  35.3 0.3 convolution_add_fusion.9
  35.6 0.3 convolution_add_fusion.8
  35.8 0.3 convolution_add_fusion.7
  36.1 0.3 convolution_add_fusion.6
  36.4 0.3 convolution_add_fusion.5
  36.6 0.7 add_bitcast_fusion
  37.3 0.8 copy.10
  38.1 3.4 all-to-all-start
  41.5 5.8 %all_gather.7 = f32[2,256,128]{2,1,0:T(8,128)S(1)} all-gather(f32[2,128,128]{2,1,0:T(8,128)S(1)} %get-tuple-element.16), channel_id=1, replica_groups=mesh['slab'=16,'grp'=2] {'grp'}, dimensions={1}, use_global_device_ids=true | all-gather | bytes 393216 | tf_op jit(solution)/shard_map/all_gather | solution.py:76
  47.8 4.8 %multiply_add_fusion = (f32[128,64,128]{2,1,0:T(8,128)S(1)}, f32[128,64,128]{2,1,0:T(8,128)S(1)}, f32[128,64,128]{2,1,0:T(8,128)S(1)}, f32[128,64,128]{2,1,0:T(8,128)S(1)}) fusion(f32[128,128]{1,0:T(8,128)S(1)} %get-tuple-element.10, f32[128,64]{1,0:T(8,128)S(1)} %copy.16, f32[128,128]{1,0:T(8,128)S(1)} %get-tuple-element.11, f32[128,64]{1,0:T(8,128)S(1)} %copy.15, ...), kind=kLoop, calls=%fused_computation.22 | loop fusion | flops 12582912 | bytes 17170432 | tf_op jit(solution)/shard_map/add | solution.py:92
  52.7 6.2 %fusion = f32[128,8192]{1,0:T(8,128)S(1)} fusion(f32[16,8,64,128]{3,2,1,0:T(8,128)S(1)} %bitcast.118), kind=kOutput, calls=%fused_computation.6 | convolution fusion | flops 1610858496 | bytes 8388608 | tf_op jit(solution)/shard_map/dot_general | solution.py:23
  58.9 6.4 %fusion.4 = f32[128,8192]{1,0:T(8,128)S(1)} fusion(f32[16,8,64,128]{3,2,1,0:T(8,128)S(1)} %bitcast.120), kind=kOutput, calls=%fused_computation.10 | convolution fusion | flops 1610858496 | bytes 8388608 | tf_op jit(solution)/shard_map/dot_general | solution.py:23
  65.3 6.3 %convolution_subtract_fusion = f32[128,8192]{1,0:T(8,128)S(1)} fusion(f32[128,8192]{1,0:T(8,128)S(1)} %fusion, f32[16,8,64,128]{3,2,1,0:T(8,128)S(1)} %bitcast.121), kind=kOutput, calls=%fused_computation | convolution fusion | flops 1611907072 | bytes 12582912 | tf_op jit(solution)/shard_map/dot_general | solution.py:23
  71.6 6.5 %convolution_add_fusion = f32[128,8192]{1,0:T(8,128)S(1)} fusion(f32[128,8192]{1,0:T(8,128)S(1)} %fusion.4, f32[16,8,64,128]{3,2,1,0:T(8,128)S(1)} %bitcast.119), kind=kOutput, calls=%fused_computation.1 | convolution fusion | flops 1611907072 | bytes 12582912 | tf_op jit(solution)/shard_map/dot_general | solution.py:23
  78.1 6.0 %fusion.6 = f32[128,8192]{1,0:T(8,128)S(1)} fusion(f32[16,8,64,128]{3,2,1,0:T(8,128)S(1)} %bitcast.114), kind=kOutput, calls=%fused_computation.12 | convolution fusion | flops 1610858496 | bytes 8388608 | tf_op jit(solution)/shard_map/dot_general | solution.py:23
  84.1 9.3 %fusion.10 = f32[128,8192]{1,0:T(8,128)} fusion(f32[16,8,64,128]{3,2,1,0:T(8,128)S(1)} %bitcast.116), kind=kOutput, calls=%fused_computation.16 | convolution fusion | flops 1610858496 | bytes 8388608 | tf_op jit(solution)/shard_map/dot_general | solution.py:23
  93.4 6.4 %convolution_subtract_fusion.1 = f32[128,8192]{1,0:T(8,128)S(1)} fusion(f32[128,8192]{1,0:T(8,128)S(1)} %fusion.6, f32[16,8,64,128]{3,2,1,0:T(8,128)S(1)} %bitcast.117), kind=kOutput, calls=%fused_computation.2 | convolution fusion | flops 1611907072 | bytes 12582912 | tf_op jit(solution)/shard_map/dot_general | solution.py:23
  99.7 16.3 %multiply_bitcast_fusion.1 = (f32[16,8,64,128]{3,1,2,0:T(8,128)}, f32[16,8,64,128]{3,1,2,0:T(8,128)}, f32[16,8,64,128]{3,1,2,0:T(8,128)}) fusion(f32[128]{0:T(128)S(1)} %get-tuple-element.23, f32[128]{0:T(128)S(1)} %get-tuple-element.24, f32[128,8192]{1,0:T(8,128)S(1)} %convolution_subtract_fusion.1, f32[128,8192]{1,0:T(8,128)S(1)} %convolution_subtract_fusion, ...), kind=kOutput, calls=%fused_computation.19 | convolution fusion | flops 1630781440 | bytes 33555456 | tf_op jit(solution)/shard_map/dot_general | solution.py:23
  116.0 4.9 %copy.24 = f32[16,8,64,128]{3,2,1,0:T(8,128)} copy(f32[16,8,64,128]{3,1,2,0:T(8,128)} %get-tuple-element.4) | data formatting | bytes 8388608
  120.9 0.3 reduce-scatter.5.cloned.1.call-start
  121.2 3.1 copy.25
  124.3 0.7 copy-done
  125.0 0.7 copy.26
  125.8 1.7 pad_maximum_fusion
  127.5 1.7 copy.17
  129.1 9.8 %copy.66 = f32[16,8,128,128]{3,1,2,0:T(8,128)} copy(f32[16,8,128,128]{3,2,1,0:T(8,128)S(1)} %bitcast.123) | data formatting | bytes 16777216
  138.9 91.2 %all-reduce.3.cloned.1.call-done = f32[128,64,128]{2,1,0:T(8,128)} async-done(((f32[128,64,128]{2,1,0:T(8,128)}), f32[128,64,128]{2,1,0:T(8,128)}) %all-reduce.3.cloned.1.call-update) | async-done | bytes 4194320 | tf_op jit(solution)/shard_map/pmax | solution.py:121
  230.1 1.7 constant_dynamic-slice_fusion
  231.8 105.0 %reduce-scatter.5.cloned.1.call-done = f32[8,16384]{1,0:T(8,128)} async-done(((f32[128,16384]{1,0:T(8,128)}), f32[8,16384]{1,0:T(8,128)}) %reduce-scatter.5.cloned.1.call-update) | async-done | bytes 524304
  336.8 1.9 copy.18
  (21 shorter events, 1.0 us)
Async XLA Ops:
  7.9 23.7 %collective-permute-start = (f32[2,192]{1,0:T(2,128)S(1)}, f32[2,192]{1,0:T(2,128)S(1)}, u32[]{:S(2)}, u32[]{:S(2)}) collective-permute-start(f32[2,192]{1,0:T(2,128)S(1)} %slice.81), channel_id=1, source_target_pairs={{0,1},{1,2},{2,3},{3,4},{4,5},{5,6},{6,7},{7,8},{8,9},{9,10},{10,1... | collective-permute-start | bytes 4616 | tf_op jit(solution)/shard_map/ppermute | solution.py:19
  38.1 9.3 %all-to-all-start = ((f32[2,128,128]{1,0,2:T(2,128)}), f32[2,128,128]{1,0,2:T(2,128)S(1)}, u32[]{:S(2)}, u32[]{:S(2)}) async-start(f32[2,128,128]{1,0,2:T(2,128)} %copy.10), calls=%async_computation | async-start | bytes 262144 | tf_op jit(solution)/shard_map/all_to_all | solution.py:75
  41.5 188.7 %all-reduce.3.cloned.1.call-start = ((), (), s32[]{:S(2)}) async-start(), calls=%async_computation.2 | async-start | bytes 8388608 | tf_op jit(solution)/shard_map/pmax | solution.py:121
  120.9 215.9 %reduce-scatter.5.cloned.1.call-start = ((), (), s32[]{:S(2)}) async-start(), calls=%async_computation.3 | async-start | bytes 8912896
  121.2 3.8 %copy-start = (f32[16,8,64,128]{3,1,2,0:T(8,128)S(1)}, f32[16,8,64,128]{3,1,2,0:T(8,128)}, u32[]{:S(2)}) copy-start(f32[16,8,64,128]{3,1,2,0:T(8,128)} %get-tuple-element.3) | copy-start | bytes 12582916
Sparse Core Ops, SparseCore 0:
  121.0 109.0 all-reduce.2
  234.2 102.5 reduce-scatter.4
where the time goes:
time: 352 us; the launch traced here: 346 us
  waiting for transfers between devices  196 us (56%)
  matrix products  67.8 us (19%)
  local copies, waits for them, and re-layouts  28.5 us (8%)
  blocking collectives  18.1 us (5%)
  between operations  16.9 us (5%)
  other arithmetic  9.95 us (3%)
  starting transfers between devices  8.6 us (2%)
    unnamed x3, waiting for transfers between devices  105 us
    pmax x1, waiting for transfers between devices, on_device(): every_held = lax.pmax(largest, 'slab')  91.2 us
    dot_general x24, matrix products, matmul_exact(): jnp.dot(left_side, right_side, precision=lax.Precision.HIGHEST, preferred...  67.8 us
    unnamed x11, local copies, waits for them, and re-layouts  24.8 us
    unnamed x1, blocking collectives  12.3 us
  transfers between devices with their start and end apart: 4, of which 2 were waited for; matrix products, arithmetic and copies ran while one was open for 7% of the time, Pallas kernels for 0%

commit v1 on v0

v1 whole, which is shorter than its diff:
```python
import functools
import math

import jax
import jax.numpy as jnp
import numpy as np
from jax import lax
from jax.experimental import pallas as pl
from jax.experimental.pallas import tpu as pltpu
from jax.sharding import PartitionSpec as P

NCH = 256
HOP = 64
KW = 128
LW = 128
Q = 128
BLOCKS = 2
LANES = 128


def split_np(table):
    hi = table.astype(jnp.bfloat16)
    lo = (table - hi.astype(np.float64)).astype(jnp.bfloat16)
    return jnp.asarray(hi), jnp.asarray(lo)


def split(values):
    hi = values.astype(jnp.bfloat16)
    lo = (values - hi.astype(jnp.float32)).astype(jnp.bfloat16)
    return hi, lo


def dft_tables():
    i = np.arange(NCH)
    w = 0.5 - 0.5 * np.cos(2.0 * np.pi * i / NCH)
    w = w / np.sqrt(np.sum(w * w))
    turns = (i[:, None] * i[None, :] % NCH) * (2.0 * np.pi / NCH)
    cos, sin = w[:, None] * np.cos(turns), w[:, None] * np.sin(turns)
    to_real = np.concatenate([cos, sin], 0)
    to_imag = np.concatenate([-sin, cos], 0)
    return to_real, to_imag


def dot3(a_hi, a_lo, b_hi, b_lo, dims):
    dot = functools.partial(
        lax.dot_general, dimension_numbers=(dims, ((), ())), preferred_element_type=jnp.float32
    )
    return dot(a_hi, b_hi) + dot(a_lo, b_hi) + dot(a_hi, b_lo)


def surfaces(
    blk, prev, ty_hi, ty_lo, tx_hi, tx_lo, phy, phx, phq, held, coh, ext, a_hi, a_lo, *, own_bins, own_w, slabs
):
    n = pl.program_id(0)
    rows = Q // 2
    lane = lax.broadcasted_iota(jnp.int32, (rows, LANES), 1)
    low = lane < HOP

    @pl.when(n == 0)
    def _():
        held[...] = jnp.zeros_like(held)
        coh[...] = jnp.zeros_like(coh)
        ext[:, 0:8, :] = jnp.zeros((2, 8, LANES), jnp.float32)

    @pl.when(n > 0)
    def _():
        ext[:, 0:8, :] = prev[0, :, rows - 8 :, :]

    for b in range(BLOCKS):
        ext[:, 8 + b * rows : 8 + (b + 1) * rows, :] = blk[b]
    frames_hi, frames_lo = [], []
    for b in range(BLOCKS):
        at = 8 + b * rows
        even, odd = [], []
        for c in range(2):
            r0 = ext[c, at : at + rows, :]
            r1 = ext[c, at - 1 : at - 1 + rows, :]
            r2 = ext[c, at - 2 : at - 2 + rows, :]
            even += [
                pltpu.roll(jnp.where(low, r1, r2), HOP, 1),
                pltpu.roll(jnp.where(low, r0, r1), HOP, 1),
            ]
            odd += [r1, r0]
        for part in (even, odd):
            hi, lo = split(jnp.concatenate(part, axis=1))
            frames_hi.append(hi)
            frames_lo.append(lo)
    f_hi = jnp.concatenate(frames_hi, axis=0)
    f_lo = jnp.concatenate(frames_lo, axis=0)
    upper = dot3(f_hi, f_lo, ty_hi[...], ty_lo[...], ((1,), (0,)))
    lower = dot3(tx_hi[...], tx_lo[...], f_hi, f_lo, ((1,), (1,)))

    phy_c = [jnp.concatenate([phy[0, p, 0]] * (rows // 8), axis=0) for p in range(2)]
    phy_s = [jnp.concatenate([phy[0, p, 1]] * (rows // 8), axis=0) for p in range(2)]
    for b in range(BLOCKS):
        right = [[], [], [], []]
        for p in range(2):
            part = upper[(2 * b + p) * rows : (2 * b + p + 1) * rows]
            yr, yi = part[:, :LW], part[:, LW:]
            zr = yr * phy_c[p] - yi * phy_s[p]
            zi = yr * phy_s[p] + yi * phy_c[p]
            right[0].append(zr)
            right[1].append(zi)
        zr = jnp.concatenate(right[0], axis=0)
        zi = jnp.concatenate(right[1], axis=0)
        zr_hi, zr_lo = split(zr)
        zi_hi, zi_lo = split(zi)

        def weights(zr, zi):
            return jnp.concatenate(
                [jnp.concatenate([zr, -zi], 1), jnp.concatenate([zi, zr], 1)], axis=0
            )

        y_hi, y_lo = weights(zr_hi, zi_hi), weights(zr_lo, zi_lo)
        xr = lower[:own_w, b * Q : (b + 1) * Q]
        xi = lower[own_w:, b * Q : (b + 1) * Q]
        ur = xr * phx[0, 0] - xi * phx[0, 1]
        ui = xr * phx[0, 1] + xi * phx[0, 0]
        for q in range(own_bins):
            c = phq[0, 0, q : q + 1, :]
            s = phq[0, 1, q : q + 1, :]
            hi, lo = split(jnp.concatenate([ur * c - ui * s, ur * s + ui * c], axis=1))
            a_hi[q * own_w : (q + 1) * own_w, :] = hi
            a_lo[q * own_w : (q + 1) * own_w, :] = lo
        surf = dot3(a_hi[...], a_lo[...], y_hi, y_lo, ((1,), (0,)))
        sr = surf[:, :LW].reshape(own_bins, own_w, LW)
        si = surf[:, LW:].reshape(own_bins, own_w, LW)
        coh[0] += sr
        coh[1] += si
        held[...] = jnp.maximum(held[...], sr * sr + si * si)

    @pl.when(n == pl.num_programs(0) - 1)
    def _():
        held[...] = jnp.sqrt(held[...])
        coh[...] = coh[...] * (1.0 / math.sqrt(slabs * BLOCKS))


def on_device(capture, dropped):
    slab_count = lax.axis_size("slab")
    group_count = lax.axis_size("grp")
    slab = lax.axis_index("slab")
    grp = lax.axis_index("grp")
    own_bins = Q // slab_count
    own_w = KW // group_count
    rows = Q // 2
    local = capture.reshape(2, capture.shape[1] // LANES, LANES)
    every = lax.all_gather(local, ("slab", "grp"), axis=0, tiled=False)
    every = every.reshape(-1, 2, every.shape[2], LANES)
    every = every.reshape(every.shape[0], 2, -1, rows, LANES).swapaxes(1, 2)
    every = every.reshape(slab_count * BLOCKS, 2, rows, LANES)
    drops = lax.all_gather(dropped, "slab", axis=0, tiled=True)
    period = Q * HOP
    stamps = jnp.arange(slab_count, dtype=jnp.int32) * (BLOCKS * period) + jnp.cumsum(drops).astype(
        jnp.int32
    )

    to_real, to_imag = dft_tables()
    ty = np.concatenate([to_real[:, KW:], to_imag[:, KW:]], 1)
    tx = np.stack(
        [
            np.concatenate(
                [to_real[:, g * own_w : (g + 1) * own_w], to_imag[:, g * own_w : (g + 1) * own_w]], 1
            ).T
            for g in range(group_count)
        ]
    ) / math.sqrt(Q)
    ty_hi, ty_lo = split_np(ty)
    tx_hi, tx_lo = (lax.dynamic_index_in_dim(t, grp, 0, False) for t in split_np(tx))

    def turn(k, period):
        a = (k % period).astype(jnp.float32) * (2.0 * math.pi / period)
        return jnp.cos(a), -jnp.sin(a)

    st = stamps[:, None, None]
    j = np.concatenate([np.arange(0, Q, 2), np.arange(1, Q, 2)]).astype(np.int32)
    bins = slab * own_bins + jnp.arange(own_bins, dtype=jnp.int32)
    c, s = turn(bins[None, :, None] * ((st % period + HOP * j[None, None, :]) % period), period)
    phq = jnp.stack([c, s], 1)
    k = grp * own_w + jnp.arange(own_w, dtype=jnp.int32)
    c, s = turn(k[None, :, None] * ((st + HOP * j[None, None, :]) % NCH), NCH)
    phx = jnp.stack([c, s], 1)
    ch = KW + jnp.arange(LW, dtype=jnp.int32)
    jj = jnp.stack([jnp.arange(8) * 2, jnp.arange(8) * 2 + 1]).astype(jnp.int32)
    c, s = turn(
        ch[None, None, None, :] * ((st[..., None] + HOP * jj[None, :, :, None]) % NCH), NCH
    )
    phy = jnp.stack([c, s], 2)

    whole = lambda shape: pl.BlockSpec(shape, lambda n: (0,) * len(shape))
    slabwise = lambda shape: pl.BlockSpec(shape, lambda n: (n,) + (0,) * (len(shape) - 1))
    held, coherent = pl.pallas_call(
        functools.partial(surfaces, own_bins=own_bins, own_w=own_w, slabs=slab_count),
        grid=(slab_count,),
        out_shape=[
            jax.ShapeDtypeStruct((own_bins, own_w, LW), jnp.float32),
            jax.ShapeDtypeStruct((2, own_bins, own_w, LW), jnp.float32),
        ],
        in_specs=[
            slabwise((BLOCKS, 2, rows, LANES)),
            pl.BlockSpec(
                (1, 2, rows, LANES), lambda n: (jnp.maximum(n * BLOCKS - 1, 0), 0, 0, 0)
            ),
            whole((2 * NCH, 2 * LW)),
            whole((2 * NCH, 2 * LW)),
            whole((2 * own_w, 2 * NCH)),
            whole((2 * own_w, 2 * NCH)),
            slabwise((1, 2, 2, 8, LW)),
            slabwise((1, 2, own_w, Q)),
            slabwise((1, 2, own_bins, Q)),
        ],
        out_specs=[whole((own_bins, own_w, LW)), whole((2, own_bins, own_w, LW))],
        scratch_shapes=[
            pltpu.VMEM((2, 8 + BLOCKS * rows, LANES), jnp.float32),
            pltpu.VMEM((own_bins * own_w, 2 * Q), jnp.bfloat16),
            pltpu.VMEM((own_bins * own_w, 2 * Q), jnp.bfloat16),
        ],
    )(every, every, ty_hi, ty_lo, tx_hi, tx_lo, phy, phx, phq)
    return held, coherent


def solution(mesh):
    in_specs = (P(None, ("slab", "grp")), P("slab"))
    out_specs = (P("slab", "grp", None), P(None, "slab", "grp", None))
    return jax.shard_map(
        on_device, mesh=mesh, in_specs=in_specs, out_specs=out_specs, check_vma=False
    )
```

time: 352 us -> 101 us (0.29); the launches traced: 346 us -> 101 us
  waiting for transfers between devices: 196 us -> 37.3 us
  matrix products: 67.8 us -> 0 us
  Pallas kernels: 0 us -> 23.3 us
  local copies, waits for them, and re-layouts: 28.5 us -> 5.25 us
  starting transfers between devices: 8.6 us -> 0.04 us
  blocking collectives: 18.1 us -> 13.7 us
    unnamed x3 -> x1, waiting for transfers between devices: 105 us -> 0.02 us
    pmax x1 -> x0, waiting for transfers between devices: 91.2 us -> none  [on_device(): every_held = lax.pmax(largest, 'slab')]
    dot_general x24 -> x0, matrix products: 67.8 us -> none  [matmul_exact(): jnp.dot(left_side, right_side, precision=lax.Precision.HIGHEST, preferred...]
    all_gather x0 -> x1, waiting for transfers between devices: none -> 37.3 us  [on_device(): every = lax.all_gather(local, ('slab', 'grp'), axis=0, tiled=False)]
    pallas_call x0 -> x1, Pallas kernels: none -> 23.3 us  [on_device(): pl.pallas_call(functools.partial(surfaces, own_bins=own_bins, own_w=own_w...]
    unnamed x11 -> x4, local copies, waits for them, and re-layouts: 24.8 us -> 3.47 us
    all_gather x1 -> x0, blocking collectives: 5.81 us -> none  [on_device(): upper_bank = lax.all_gather(shifted[:, :, KW:], 'grp', axis=1, tiled=True)]
    ppermute x1 -> x0, starting transfers between devices: 4.89 us -> none  [passed_along(): return lax.ppermute(array, axis, pairs)]
  transfers between devices with their start and end apart: 4 -> 1, of which waited for: 2 -> 1; matrix products, arithmetic and copies ran while one was open for 7% -> 10% of each run, Pallas kernels for 0% -> 0%
where the time goes in v1:
time: 101 us
  waiting for transfers between devices  37.3 us (37%)
  Pallas kernels  23.3 us (23%)
  between operations  14.7 us (15%)
  blocking collectives  13.7 us (14%)
  other arithmetic  6.56 us (6%)
  local copies, waits for them, and re-layouts  5.25 us (5%)
    all_gather x1, waiting for transfers between devices, on_device(): every = lax.all_gather(local, ('slab', 'grp'), axis=0, tiled=False)  37.3 us
    pallas_call x1, Pallas kernels, on_device(): pl.pallas_call(functools.partial(surfaces, own_bins=own_bins, own_w=own_w...  23.3 us
    unnamed x1, blocking collectives  13.7 us
    unnamed x4, local copies, waits for them, and re-layouts  3.47 us
    cos x3, other arithmetic, turn(): return (jnp.cos(a), -jnp.sin(a))  3.06 us
  transfers between devices with their start and end apart: 1, of which 1 were waited for; matrix products, arithmetic and copies ran while one was open for 10% of the time, Pallas kernels for 0%

profile of v1, /device:TPU:0, one launch (start us, length us, event | category | flops | bytes accessed | tf_op | source)
XLA Modules:
  0.0 100.9 jit_solution(16470332429893260848)
XLA Ops:
  7.2 0.0 all-gather.2.cloned.1.call-start
  7.2 1.5 %copy.15 = f32[1,2,64,128]{3,2,1,0:T(8,128)} copy(f32[1,2,64,128]{3,1,2,0:T(2,128)} %bitcast.11) | data formatting | bytes 131072
  8.7 0.0 all-gather.2.cloned.1.call-update
  9.4 1.2 %dynamic-slice = u32[1]{0:T(128)} dynamic-slice(u32[32]{0:T(128)} %constant.120, u32[]{:T(128)S(6)} %add.239), dynamic_slice_sizes={1} | dynamic-slice | bytes 12
  10.6 0.8 dynamic-update-slice
  11.4 13.7 %all-reduce = s32[16]{0:T(128)S(1)} all-reduce(s32[16]{0:T(128)S(1)} %dynamic-update-slice), channel_id=1, replica_groups=mesh['slab'=16,'grp'=2] {'slab'}, use_global_device_ids=true, to_apply=%add | all-reduce | flops 16 | bytes 128
  25.1 0.1 copy.12
  25.2 0.1 reduce
  25.4 0.7 add_select_fusion.5
  26.2 0.3 fusion.11
  26.5 0.7 pad_maximum_fusion.2.phq
  27.1 0.1 and_select_fusion
  27.2 0.6 fusion.10
  27.8 0.7 pad_maximum_fusion.1.phy
  28.6 1.7 %dynamic-slice_bitcast_fusion = (bf16[128,512]{1,0:T(8,128)(2,1)}, bf16[128,512]{1,0:T(8,128)(2,1)}) fusion(bf16[2,128,512]{2,1,0:T(8,128)(2,1)} %constant.114.clone, s32[]{:T(128)S(6)} %select_n.99, bf16[2,128,512]{2,1,0:T(8,128)(2,1)} %constant.113.clone), kind=kLoop, calls=%fused_computation.22 | loop fusion | bytes 524292 | tf_op jit(solution)/shard_map/jit(dynamic_index_in_dim)/squeeze | solution.py:168
  30.3 2.1 %fusion.3 = (f32[16,1,64,128]{3,2,1,0:T(8,128)S(1)}, f32[16,1,64,128]{3,2,1,0:T(8,128)S(1)}) fusion(s32[16,128]{1,0:T(8,128)S(1)} %get-tuple-element.9, s32[64]{0:T(128)S(1)} %iota_add_fusion.1), kind=kLoop, calls=%fused_computation.11 | loop fusion | flops 1966080 | bytes 1057024 | tf_op jit(solution)/shard_map/cos | solution.py:172
  32.4 1.1 %pad_maximum_fusion.phx = f32[16,2,64,128]{3,2,1,0:T(8,128)} fusion(f32[16,1,64,128]{3,2,1,0:T(8,128)S(1)} %get-tuple-element.7, f32[16,1,64,128]{3,2,1,0:T(8,128)S(1)} %get-tuple-element.6), kind=kLoop, calls=%fused_computation | loop fusion | flops 262144 | bytes 2097152 | tf_op jit(solution)/shard_map/stack | solution.py:181
  33.5 37.3 %all-gather.2.cloned.1.call-done.blk.prev = f32[32,2,64,128]{3,2,1,0:T(8,128)} async-done(((f32[1,2,64,128]{3,2,1,0:T(8,128)}), f32[32,2,64,128]{3,2,1,0:T(8,128)}) %all-gather.2.cloned.1.call-update) | async-done | bytes 2097168 | tf_op jit(solution)/shard_map/all_gather | solution.py:147
  70.8 23.3 %shard_map.95 = (f32[8,64,128]{2,1,0:T(8,128)}, f32[2,8,64,128]{3,2,1,0:T(8,128)}) custom-call(f32[32,2,64,128]{3,2,1,0:T(8,128)} %all-gather.2.cloned.1.call-done.blk.prev, f32[32,2,64,128]{3,2,1,0:T(8,128)} %all-gather.2.cloned.1.call-done.blk.prev, bf16[512,256]{1,0:T(8,128)(2,1)} %constant.111.clone.ty_hi, bf16[512,256]{1,0:T(8,128)(2,1)} %constant.112.clone.ty_lo, ...), custom_call_target="tpu_custom_call" | custom-call | tf_op jit(solution)/shard_map/pallas_call | solution.py:191
  (8 shorter events, 0.1 us)
Async XLA Ops:
  7.2 63.6 %all-gather.2.cloned.1.call-start = ((), (), s32[]{:S(2)}) async-start(), calls=%async_computation | async-start | bytes 2162688 | tf_op jit(solution)/shard_map/all_gather | solution.py:147
Sparse Core Ops, SparseCore 0:
  11.6 59.1 all-gather.1

commit v2 on v1

v2 whole, which is shorter than its diff:
```python
import functools
import math

import jax
import jax.numpy as jnp
import numpy as np
from jax import lax
from jax.experimental import pallas as pl
from jax.experimental.pallas import tpu as pltpu
from jax.sharding import PartitionSpec as P

NCH = 256
HOP = 64
KW = 128
LW = 128
Q = 128
BLOCKS = 2
LANES = 128


def split_np(table):
    hi = table.astype(jnp.bfloat16)
    lo = (table - hi.astype(np.float64)).astype(jnp.bfloat16)
    return jnp.asarray(hi), jnp.asarray(lo)


def split(values):
    hi = values.astype(jnp.bfloat16)
    lo = (values - hi.astype(jnp.float32)).astype(jnp.bfloat16)
    return hi, lo


def dft_tables():
    i = np.arange(NCH)
    w = 0.5 - 0.5 * np.cos(2.0 * np.pi * i / NCH)
    w = w / np.sqrt(np.sum(w * w))
    turns = (i[:, None] * i[None, :] % NCH) * (2.0 * np.pi / NCH)
    cos, sin = w[:, None] * np.cos(turns), w[:, None] * np.sin(turns)
    to_real = np.concatenate([cos, sin], 0)
    to_imag = np.concatenate([-sin, cos], 0)
    return to_real, to_imag


def dot3(a_hi, a_lo, b_hi, b_lo, dims):
    dot = functools.partial(
        lax.dot_general, dimension_numbers=(dims, ((), ())), preferred_element_type=jnp.float32
    )
    return dot(a_hi, b_hi) + dot(a_lo, b_hi) + dot(a_hi, b_lo)


def cos_turns(turns, period):
    v = (jnp.abs(turns.astype(jnp.float32) * (1.0 / period) - 0.5) - 0.25) * (2.0 * math.pi)
    v2 = v * v
    total = jnp.full_like(v, 1.0 / math.factorial(13))
    for order in (11, 9, 7, 5, 3, 1):
        sign = 1.0 if order % 4 == 1 else -1.0
        total = total * v2 + sign / math.factorial(order)
    return total * v


def rotation(turns, period):
    return cos_turns(turns & (period - 1), period), cos_turns((turns + period // 4) & (period - 1), period)


def surfaces(
    own_blk, own_drop, ty_hi, ty_lo, tx_hi, tx_lo, held, coh,
    buf, drops, ext, a_hi, a_lo, send_sem, fwd_sem, recv_sem, dsend_sem, drecv_sem,
    *, slabs, groups, own_bins, own_w
):
    slab, grp = lax.axis_index("slab"), lax.axis_index("grp")
    partner = slab + 1 - 2 * (slab % 2)
    half = slabs // 2
    rows = Q // 2
    local = own_blk.shape[1]
    period = Q * HOP

    barrier = pltpu.get_barrier_semaphore()

    def greet(i, carry):
        pl.semaphore_signal(
            barrier,
            inc=1,
            device_id=((slab + i // groups) % slabs, (grp + i % groups) % groups),
            device_id_type=pl.DeviceIdType.MESH,
        )
        return carry

    lax.fori_loop(1, slabs * groups, greet, 0)

    def to_direct(i):
        return pltpu.make_async_remote_copy(
            src_ref=own_blk,
            dst_ref=buf.at[slab, grp],
            send_sem=send_sem.at[i],
            recv_sem=recv_sem.at[slab, grp],
            device_id=((slab + 2 * (i // groups)) % slabs, (grp + i % groups) % groups),
            device_id_type=pl.DeviceIdType.MESH,
        )

    def drop_copy(i):
        return pltpu.make_async_remote_copy(
            src_ref=own_drop,
            dst_ref=drops.at[slab],
            send_sem=dsend_sem.at[i],
            recv_sem=drecv_sem.at[slab],
            device_id=((slab + i) % slabs, grp),
            device_id_type=pl.DeviceIdType.MESH,
        )

    def arrival(origin, g):
        return pltpu.make_async_remote_copy(
            src_ref=own_blk,
            dst_ref=buf.at[origin, g],
            send_sem=send_sem.at[0],
            recv_sem=recv_sem.at[origin, g],
            device_id=(partner, grp),
            device_id_type=pl.DeviceIdType.MESH,
        )

    def drop_arrival(origin):
        return pltpu.make_async_remote_copy(
            src_ref=own_drop,
            dst_ref=drops.at[origin],
            send_sem=dsend_sem.at[0],
            recv_sem=drecv_sem.at[origin],
            device_id=(partner, grp),
            device_id_type=pl.DeviceIdType.MESH,
        )

    def onward(e, dg):
        origin, g = (slab - 2 * e + slabs) % slabs, (grp + dg) % groups
        return pltpu.make_async_remote_copy(
            src_ref=buf.at[origin, g],
            dst_ref=buf.at[origin, g],
            send_sem=fwd_sem.at[e, dg],
            recv_sem=recv_sem.at[origin, g],
            device_id=(partner, grp),
            device_id_type=pl.DeviceIdType.MESH,
        )

    def own_onward():
        return pltpu.make_async_remote_copy(
            src_ref=own_blk,
            dst_ref=buf.at[slab, grp],
            send_sem=fwd_sem.at[0, 0],
            recv_sem=recv_sem.at[slab, grp],
            device_id=(partner, grp),
            device_id_type=pl.DeviceIdType.MESH,
        )

    def relay(e, first):
        origin = (slab - 2 * e + slabs) % slabs
        for dg in range(first, groups):
            arrival(origin, (grp + dg) % groups).wait_recv()
            onward(e, dg).start()

    drops[slab] = own_drop[...]
    buf[slab, grp] = own_blk[...]
    held[...] = jnp.zeros_like(held)
    coh[...] = jnp.zeros_like(coh)
    pl.semaphore_wait(barrier, slabs * groups - 1)

    def run(copy_of, first, last, act):
        def body(i, carry):
            act(copy_of(i))
            return carry

        lax.fori_loop(first, last, body, 0)

    run(drop_copy, 1, slabs, lambda copy: copy.start())
    own_onward().start()
    run(to_direct, 1, half * groups, lambda copy: copy.start())
    relay(0, 1)
    run(lambda i: drop_arrival((slab + i) % slabs), 1, slabs, lambda copy: copy.wait_recv())
    relay(1, 0)

    lane = lax.broadcasted_iota(jnp.int32, (rows, LANES), 1)
    low = lane < HOP
    jlane = lax.broadcasted_iota(jnp.int32, (8, Q), 1)
    jlane = 2 * (jlane & (rows - 1)) + (jlane >= rows).astype(jnp.int32)
    bins = slab * own_bins + lax.broadcasted_iota(jnp.int32, (own_bins, Q), 0)
    kchan = grp * own_w + lax.broadcasted_iota(jnp.int32, (own_w, Q), 0)
    lchan = KW + lax.broadcasted_iota(jnp.int32, (8, LW), 1)
    jsub = 2 * lax.broadcasted_iota(jnp.int32, (8, LW), 0)

    def spread(array, count):
        return jnp.concatenate([array[:1]] * count, axis=0)

    def step(t, carry):
        n = (slab - t + slabs) % slabs
        before = (n - 1 + slabs) % slabs

        @pl.when((t % 2 == 0) & (t // 2 + 2 < half))
        def _():
            relay(t // 2 + 2, 0)

        @pl.when(t % 2 == 0)
        def _():
            for g in range(groups):
                arrival(before, g).wait_recv()

        stamp = jnp.zeros((8, LANES), jnp.int32) + n * (BLOCKS * period)
        for other in range(slabs):
            stamp = stamp + drops[other] * jnp.where(other <= n, 1, 0)
        at_j = stamp + HOP * jlane
        phq = rotation(bins * (spread(at_j, own_bins) & (period - 1)), period)
        phx = rotation(kchan * (spread(at_j, own_w) & (NCH - 1)), NCH)
        phy = [rotation(lchan * ((stamp + HOP * (jsub + p)) & (NCH - 1)), NCH) for p in range(2)]

        ext[:, 0:8, :] = buf[before, groups - 1, :, local - 8 :, :] * jnp.where(n > 0, 1.0, 0.0)
        for g in range(groups):
            ext[:, 8 + g * local : 8 + (g + 1) * local, :] = buf[n, g]
        frames_hi, frames_lo = [], []
        for b in range(BLOCKS):
            at = 8 + b * rows
            even, odd = [], []
            for c in range(2):
                r0 = ext[c, at : at + rows, :]
                r1 = ext[c, at - 1 : at - 1 + rows, :]
                r2 = ext[c, at - 2 : at - 2 + rows, :]
                even += [
                    pltpu.roll(jnp.where(low, r1, r2), HOP, 1),
                    pltpu.roll(jnp.where(low, r0, r1), HOP, 1),
                ]
                odd += [r1, r0]
            for part in (even, odd):
                hi, lo = split(jnp.concatenate(part, axis=1))
                frames_hi.append(hi)
                frames_lo.append(lo)
        f_hi = jnp.concatenate(frames_hi, axis=0)
        f_lo = jnp.concatenate(frames_lo, axis=0)
        upper = dot3(f_hi, f_lo, ty_hi[...], ty_lo[...], ((1,), (0,)))
        lower = dot3(tx_hi[...], tx_lo[...], f_hi, f_lo, ((1,), (1,)))

        phy_c = [jnp.concatenate([phy[p][0]] * (rows // 8), axis=0) for p in range(2)]
        phy_s = [jnp.concatenate([phy[p][1]] * (rows // 8), axis=0) for p in range(2)]
        for b in range(BLOCKS):
            zrs, zis = [], []
            for p in range(2):
                part = upper[(2 * b + p) * rows : (2 * b + p + 1) * rows]
                yr, yi = part[:, :LW], part[:, LW:]
                zrs.append(yr * phy_c[p] - yi * phy_s[p])
                zis.append(yr * phy_s[p] + yi * phy_c[p])
            zr_hi, zr_lo = split(jnp.concatenate(zrs, axis=0))
            zi_hi, zi_lo = split(jnp.concatenate(zis, axis=0))

            def weights(zr, zi):
                return jnp.concatenate(
                    [jnp.concatenate([zr, -zi], 1), jnp.concatenate([zi, zr], 1)], axis=0
                )

            y_hi, y_lo = weights(zr_hi, zi_hi), weights(zr_lo, zi_lo)
            xr = lower[:own_w, b * Q : (b + 1) * Q]
            xi = lower[own_w:, b * Q : (b + 1) * Q]
            ur = xr * phx[0] - xi * phx[1]
            ui = xr * phx[1] + xi * phx[0]
            for q in range(own_bins):
                c = phq[0][q : q + 1, :]
                s = phq[1][q : q + 1, :]
                hi, lo = split(jnp.concatenate([ur * c - ui * s, ur * s + ui * c], axis=1))
                a_hi[q * own_w : (q + 1) * own_w, :] = hi
                a_lo[q * own_w : (q + 1) * own_w, :] = lo
            surf = dot3(a_hi[...], a_lo[...], y_hi, y_lo, ((1,), (0,)))
            sr = surf[:, :LW].reshape(own_bins, own_w, LW)
            si = surf[:, LW:].reshape(own_bins, own_w, LW)
            coh[0] += sr
            coh[1] += si
            held[...] = jnp.maximum(held[...], sr * sr + si * si)
        return carry

    lax.fori_loop(0, slabs, step, 0)
    held[...] = jnp.sqrt(held[...])
    coh[...] = coh[...] * (1.0 / math.sqrt(slabs * BLOCKS))

    run(drop_copy, 1, slabs, lambda copy: copy.wait_send())
    run(to_direct, 1, half * groups, lambda copy: copy.wait_send())
    own_onward().wait_send()
    run(lambda i: onward(i // groups, i % groups), 1, half * groups, lambda copy: copy.wait_send())


def on_device(capture, dropped):
    slabs = lax.axis_size("slab")
    groups = lax.axis_size("grp")
    grp = lax.axis_index("grp")
    own_bins = Q // slabs
    own_w = KW // groups
    local = capture.shape[1] // LANES
    to_real, to_imag = dft_tables()
    ty = np.concatenate([to_real[:, KW:], to_imag[:, KW:]], 1)
    tx = np.stack(
        [
            np.concatenate(
                [to_real[:, g * own_w : (g + 1) * own_w], to_imag[:, g * own_w : (g + 1) * own_w]], 1
            ).T
            for g in range(groups)
        ]
    ) / math.sqrt(Q)
    ty_hi, ty_lo = split_np(ty)
    tx_hi, tx_lo = (lax.dynamic_index_in_dim(t, grp, 0, False) for t in split_np(tx))
    dma = pltpu.SemaphoreType.DMA
    held, coherent = pl.pallas_call(
        functools.partial(surfaces, slabs=slabs, groups=groups, own_bins=own_bins, own_w=own_w),
        out_shape=[
            jax.ShapeDtypeStruct((own_bins, own_w, LW), jnp.float32),
            jax.ShapeDtypeStruct((2, own_bins, own_w, LW), jnp.float32),
        ],
        in_specs=[pl.BlockSpec(memory_space=pltpu.VMEM)] * 6,
        out_specs=[pl.BlockSpec(memory_space=pltpu.VMEM)] * 2,
        scratch_shapes=[
            pltpu.VMEM((slabs, groups, 2, local, LANES), jnp.float32),
            pltpu.VMEM((slabs, 8, LANES), jnp.int32),
            pltpu.VMEM((2, 8 + BLOCKS * Q // 2, LANES), jnp.float32),
            pltpu.VMEM((own_bins * own_w, 2 * Q), jnp.bfloat16),
            pltpu.VMEM((own_bins * own_w, 2 * Q), jnp.bfloat16),
            dma((slabs // 2 * groups,)),
            dma((slabs // 2, groups)),
            dma((slabs, groups)),
            dma((slabs,)),
            dma((slabs,)),
        ],
        compiler_params=pltpu.CompilerParams(
            collective_id=0, has_side_effects=True, vmem_limit_bytes=48 * 2**20
        ),
    )(
        capture.reshape(2, local, LANES),
        jnp.broadcast_to(dropped.reshape(1, 1), (8, LANES)),
        ty_hi, ty_lo, tx_hi, tx_lo,
    )
    return held, coherent


def solution(mesh):
    in_specs = (P(None, ("slab", "grp")), P("slab"))
    out_specs = (P("slab", "grp", None), P(None, "slab", "grp", None))
    return jax.shard_map(
        on_device, mesh=mesh, in_specs=in_specs, out_specs=out_specs, check_vma=False
    )
```

time: 101 us -> 52.5 us (0.52)
  the two profiles are of different devices: /device:TPU:0 before, /device:TPU:24 now
where the time goes in v2:
time: 52.5 us; the launch traced here: 52.3 us
  Pallas kernels  47.5 us (90%)
  local copies, waits for them, and re-layouts  3.49 us (7%)
  between operations  1.3 us (2%)
    pallas_call x1, Pallas kernels, on_device(): pl.pallas_call(functools.partial(surfaces, slabs=slabs, groups=groups, ow...  47.5 us
    unnamed x7, local copies, waits for them, and re-layouts  2.44 us

profile of v2, /device:TPU:24, one launch (start us, length us, event | category | flops | bytes accessed | tf_op | source)
XLA Modules:
  0.0 52.3 jit_solution(5096377751692961925)
XLA Ops:
  1.3 0.8 %copy.10 = f32[1,2,64,128]{3,2,1,0:T(8,128)S(1)} copy(f32[1,2,64,128]{3,1,2,0:T(2,128)} %bitcast.11) | data formatting | bytes 131072
  2.1 0.0 copy-start
  2.1 0.0 copy-start.1
  2.1 1.0 %dynamic-slice_bitcast_fusion = (bf16[128,512]{1,0:T(8,128)(2,1)S(1)}, bf16[128,512]{1,0:T(8,128)(2,1)S(1)}) fusion(bf16[2,128,512]{2,1,0:T(8,128)(2,1)} %constant.23.clone, s32[]{:T(128)S(6)} %select_n.5, bf16[2,128,512]{2,1,0:T(8,128)(2,1)} %constant.22.clone), kind=kLoop, calls=%fused_computation | loop fusion | bytes 524292 | tf_op jit(solution)/shard_map/jit(dynamic_index_in_dim)/squeeze | solution.py:299
  3.2 0.0 copy-done
  3.2 0.1 copy-done.1
  3.3 47.5 %shard_map.77 = (f32[8,64,128]{2,1,0:T(8,128)S(1)}, f32[2,8,64,128]{3,2,1,0:T(8,128)S(1)}) custom-call(f32[2,64,128]{2,1,0:T(8,128)S(1)} %bitcast.10, s32[8,128]{1,0:T(8,128)S(1)} %broadcast_in_dim.8.own_drop, bf16[512,256]{1,0:T(8,128)(2,1)S(1)} %copy-done.1, bf16[512,256]{1,0:T(8,128)(2,1)S(1)} %copy-done, bf16[128,512]{1,0:T(8,128)(2,1)S(1)} %get-tuple-element.3.tx_hi, ...), custom_call_target="tpu_custom_call" | custom-call | tf_op jit(solution)/shard_map/pallas_call | solution.py:301
  50.8 0.7 %copy.14 = f32[8,64,128]{2,1,0:T(8,128)} copy(f32[8,64,128]{2,1,0:T(8,128)S(1)} %get-tuple-element.6) | data formatting | bytes 524288
  51.5 0.8 %copy.15 = f32[2,8,64,128]{3,2,1,0:T(8,128)} copy(f32[2,8,64,128]{3,2,1,0:T(8,128)S(1)} %get-tuple-element.7) | data formatting | bytes 1048576
  (1 shorter events, 0.0 us)
Async XLA Ops:
  2.1 1.1 %copy-start = (bf16[512,256]{1,0:T(8,128)(2,1)S(1)}, bf16[512,256]{1,0:T(8,128)(2,1)}, u32[]{:S(2)}) copy-start(bf16[512,256]{1,0:T(8,128)(2,1)} %constant.21.clone.ty_lo) | copy-start | bytes 786436
  2.1 1.2 %copy-start.1 = (bf16[512,256]{1,0:T(8,128)(2,1)S(1)}, bf16[512,256]{1,0:T(8,128)(2,1)}, u32[]{:S(2)}) copy-start(bf16[512,256]{1,0:T(8,128)(2,1)} %constant.20.clone.ty_hi) | copy-start | bytes 786436

commit v3 on v2

--- a/solution.py
+++ b/solution.py
@@ -62,17 +62,29 @@
     return cos_turns(turns & (period - 1), period), cos_turns((turns + period // 4) & (period - 1), period)
 
 
+def flip(index, by, bits):
+    total = 0
+    for bit in range(bits):
+        w = 2**bit
+        total = total + ((index // w + by // w) % 2) * w
+    return total
+
+
 def surfaces(
-    own_blk, own_drop, ty_hi, ty_lo, tx_hi, tx_lo, held, coh,
-    buf, drops, ext, a_hi, a_lo, send_sem, fwd_sem, recv_sem, dsend_sem, drecv_sem,
+    own_blk, own_info, ty_hi, ty_lo, tx_hi, tx_lo, held, coh,
+    buf, infos, ext, a_hi, a_lo, line_sem, x_sem, y_sem, diag_sem, fwd_sem, recv_sem, isend_sem, irecv_sem,
     *, slabs, groups, own_bins, own_w
 ):
     slab, grp = lax.axis_index("slab"), lax.axis_index("grp")
-    partner = slab + 1 - 2 * (slab % 2)
-    half = slabs // 2
+    bits = slabs.bit_length() - 1
+    line = slabs // 4
     rows = Q // 2
     local = own_blk.shape[1]
     period = Q * HOP
+    last = groups - 1
+    partner = (flip(slab, 1, bits), grp)
+    beside = (flip(slab, 2, bits), grp)
+    across = (slab, 1 - grp)
 
     barrier = pltpu.get_barrier_semaphore()
 
@@ -80,99 +92,109 @@
         pl.semaphore_signal(
             barrier,
             inc=1,
-            device_id=((slab + i // groups) % slabs, (grp + i % groups) % groups),
+            device_id=(flip(slab, i // groups, bits), (grp + i) % groups),
             device_id_type=pl.DeviceIdType.MESH,
         )
         return carry
 
     lax.fori_loop(1, slabs * groups, greet, 0)
 
-    def to_direct(i):
+    def remote(src, dst, send, recv, target):
         return pltpu.make_async_remote_copy(
-            src_ref=own_blk,
-            dst_ref=buf.at[slab, grp],
-            send_sem=send_sem.at[i],
-            recv_sem=recv_sem.at[slab, grp],
-            device_id=((slab + 2 * (i // groups)) % slabs, (grp + i % groups) % groups),
-            device_id_type=pl.DeviceIdType.MESH,
+            src_ref=src, dst_ref=dst, send_sem=send, recv_sem=recv,
+            device_id=target, device_id_type=pl.DeviceIdType.MESH,
         )
 
-    def drop_copy(i):
-        return pltpu.make_async_remote_copy(
-            src_ref=own_drop,
-            dst_ref=drops.at[slab],
-            send_sem=dsend_sem.at[i],
-            recv_sem=drecv_sem.at[slab],
-            device_id=((slab + i) % slabs, grp),
-            device_id_type=pl.DeviceIdType.MESH,
-        )
-
-    def arrival(origin, g):
-        return pltpu.make_async_remote_copy(
-            src_ref=own_blk,
-            dst_ref=buf.at[origin, g],
-            send_sem=send_sem.at[0],
-            recv_sem=recv_sem.at[origin, g],
-            device_id=(partner, grp),
-            device_id_type=pl.DeviceIdType.MESH,
-        )
-
-    def drop_arrival(origin):
-        return pltpu.make_async_remote_copy(
-            src_ref=own_drop,
-            dst_ref=drops.at[origin],
-            send_sem=dsend_sem.at[0],
-            recv_sem=drecv_sem.at[origin],
-            device_id=(partner, grp),
-            device_id_type=pl.DeviceIdType.MESH,
-        )
-
-    def onward(e, dg):
-        origin, g = (slab - 2 * e + slabs) % slabs, (grp + dg) % groups
-        return pltpu.make_async_remote_copy(
-            src_ref=buf.at[origin, g],
-            dst_ref=buf.at[origin, g],
-            send_sem=fwd_sem.at[e, dg],
-            recv_sem=recv_sem.at[origin, g],
-            device_id=(partner, grp),
-            device_id_type=pl.DeviceIdType.MESH,
-        )
-
-    def own_onward():
-        return pltpu.make_async_remote_copy(
-            src_ref=own_blk,
-            dst_ref=buf.at[slab, grp],
-            send_sem=fwd_sem.at[0, 0],
-            recv_sem=recv_sem.at[slab, grp],
-            device_id=(partner, grp),
-            device_id_type=pl.DeviceIdType.MESH,
-        )
-
-    def relay(e, first):
-        origin = (slab - 2 * e + slabs) % slabs
-        for dg in range(first, groups):
-            arrival(origin, (grp + dg) % groups).wait_recv()
-            onward(e, dg).start()
-
-    drops[slab] = own_drop[...]
+    def moved(k, dg, send, target, own=False):
+        origin, g = flip(slab, k, bits), (grp + dg) % groups
+        src = own_blk if own else buf.at[origin, g]
+        return remote(src, buf.at[origin, g], send, recv_sem.at[origin, g], target)
+
+    def arrived(k, dg):
+        moved(k, dg, fwd_sem.at[0, 0, 0], partner).wait_recv()
+
+    def info_copy(i):
+        target = (flip(slab, i // groups, bits), (grp + i) % groups)
+        return remote(own_info, infos.at[slab], isend_sem.at[i], irecv_sem.at[slab], target)
+
+    def info_arrived(origin):
+        remote(own_info, infos.at[origin], isend_sem.at[0], irecv_sem.at[origin], partner).wait_recv()
+
+    def line_copy(kz):
+        return moved(0, 0, line_sem.at[kz], (flip(slab, 4 * kz, bits), grp), True)
+
+    def column_copies(kz, own=False):
+        return [
+            moved(4 * kz, 0, x_sem.at[kz], beside, own),
+            moved(4 * kz, 0, y_sem.at[kz], across, own),
+            moved(4 * kz, 0, fwd_sem.at[kz, 0, 0], partner, own),
+        ]
+
+    def forward(kz, kx, dg):
+        return moved(4 * kz + 2 * kx, dg, fwd_sem.at[kz, kx, dg], partner)
+
+    def diagonal_y(kz):
+        return moved(4 * kz + 2, 0, diag_sem.at[kz], across)
+
+    def diagonal_x(kz):
+        return moved(4 * kz, 1, diag_sem.at[kz], beside)
+
+    def from_line(kz):
+        arrived(4 * kz, 0)
+        for copy in column_copies(kz):
+            copy.start()
+
+    def from_x(kz):
+        arrived(4 * kz + 2, 0)
+
+        @pl.when(kz % 2 == 1)
+        def _():
+            diagonal_y(kz).start()
+
+        forward(kz, 1, 0).start()
+
+    def from_y(kz):
+        arrived(4 * kz, 1)
+
+        @pl.when(kz % 2 == 0)
+        def _():
+            diagonal_x(kz).start()
+
+        forward(kz, 0, 1).start()
+
+    def from_diagonal(kz):
+        arrived(4 * kz + 2, 1)
+        forward(kz, 1, 1).start()
+
+    def run(first, end, act):
+        def body(i, carry):
+            act(i)
+            return carry
+
+        lax.fori_loop(first, end, body, 0)
+
     buf[slab, grp] = own_blk[...]
     held[...] = jnp.zeros_like(held)
     coh[...] = jnp.zeros_like(coh)
     pl.semaphore_wait(barrier, slabs * groups - 1)
 
-    def run(copy_of, first, last, act):
-        def body(i, carry):
-            act(copy_of(i))
-            return carry
-
-        lax.fori_loop(first, last, body, 0)
-
-    run(drop_copy, 1, slabs, lambda copy: copy.start())
-    own_onward().start()
-    run(to_direct, 1, half * groups, lambda copy: copy.start())
-    relay(0, 1)
-    run(lambda i: drop_arrival((slab + i) % slabs), 1, slabs, lambda copy: copy.wait_recv())
-    relay(1, 0)
+    @pl.when(grp == last)
+    def _():
+        infos[slab] = own_info[...]
+        run(1, slabs * groups, lambda i: info_copy(i).start())
+
+    for copy in column_copies(0, True):
+        copy.start()
+    run(1, line, lambda kz: line_copy(kz).start())
+    zero = slab * 0
+    from_x(zero)
+    from_y(zero)
+    from_line(zero + 1)
+    run(1, slabs, lambda i: info_arrived(flip(slab, i, bits)))
+
+    @pl.when(grp != last)
+    def _():
+        info_arrived(slab)
 
     lane = lax.broadcasted_iota(jnp.int32, (rows, LANES), 1)
     low = lane < HOP
@@ -187,27 +209,42 @@
         return jnp.concatenate([array[:1]] * count, axis=0)
 
     def step(t, carry):
-        n = (slab - t + slabs) % slabs
+        n = flip(slab, t, bits)
         before = (n - 1 + slabs) % slabs
-
-        @pl.when((t % 2 == 0) & (t // 2 + 2 < half))
-        def _():
-            relay(t // 2 + 2, 0)
-
-        @pl.when(t % 2 == 0)
-        def _():
-            for g in range(groups):
-                arrival(before, g).wait_recv()
-
-        stamp = jnp.zeros((8, LANES), jnp.int32) + n * (BLOCKS * period)
+        kz, part = t // 4, t % 4
+
+        @pl.when((part == 0) & (kz + 2 < line))
+        def _():
+            from_line(kz + 2)
+
+        @pl.when(part == 1)
+        def _():
+            from_diagonal(kz)
+
+        @pl.when((part == 2) & (kz + 1 < line))
+        def _():
+            from_x(kz + 1)
+
+        @pl.when((part == 3) & (kz + 1 < line))
+        def _():
+            from_y(kz + 1)
+
+        @pl.when(part % 2 == 1)
+        def _():
+            arrived(t, 0)
+            arrived(t, 1)
+
+        drops = jnp.zeros((1, LANES), jnp.float32)
         for other in range(slabs):
-            stamp = stamp + drops[other] * jnp.where(other <= n, 1, 0)
+            drops = drops + infos[other, 4:5, :] * jnp.where(other <= n, 1.0, 0.0)
+        stamp = jnp.concatenate([drops.astype(jnp.int32) + n * (BLOCKS * period)] * 8, axis=0)
         at_j = stamp + HOP * jlane
         phq = rotation(bins * (spread(at_j, own_bins) & (period - 1)), period)
         phx = rotation(kchan * (spread(at_j, own_w) & (NCH - 1)), NCH)
         phy = [rotation(lchan * ((stamp + HOP * (jsub + p)) & (NCH - 1)), NCH) for p in range(2)]
 
-        ext[:, 0:8, :] = buf[before, groups - 1, :, local - 8 :, :] * jnp.where(n > 0, 1.0, 0.0)
+        for c in range(2):
+            ext[c, 6:8, :] = infos[before, 2 * c : 2 * c + 2, :] * jnp.where(n > 0, 1.0, 0.0)
         for g in range(groups):
             ext[:, 8 + g * local : 8 + (g + 1) * local, :] = buf[n, g]
         frames_hi, frames_lo = [], []
@@ -272,10 +309,20 @@
     held[...] = jnp.sqrt(held[...])
     coh[...] = coh[...] * (1.0 / math.sqrt(slabs * BLOCKS))
 
-    run(drop_copy, 1, slabs, lambda copy: copy.wait_send())
-    run(to_direct, 1, half * groups, lambda copy: copy.wait_send())
-    own_onward().wait_send()
-    run(lambda i: onward(i // groups, i % groups), 1, half * groups, lambda copy: copy.wait_send())
+    @pl.when(grp == last)
+    def _():
+        run(1, slabs * groups, lambda i: info_copy(i).wait_send())
+
+    run(1, line, lambda kz: line_copy(kz).wait_send())
+
+    def sent(kz):
+        for copy in column_copies(kz):
+            copy.wait_send()
+        diagonal_x(kz).wait_send()
+        for kx, dg in ((0, 1), (1, 0), (1, 1)):
+            forward(kz, kx, dg).wait_send()
+
+    run(0, line, sent)
 
 
 def on_device(capture, dropped):
@@ -297,6 +344,10 @@
     ) / math.sqrt(Q)
     ty_hi, ty_lo = split_np(ty)
     tx_hi, tx_lo = (lax.dynamic_index_in_dim(t, grp, 0, False) for t in split_np(tx))
+    blocks = capture.reshape(2, local, LANES)
+    tail = capture[:, capture.shape[1] - 2 * LANES :].reshape(4, LANES)
+    drop = jnp.broadcast_to(dropped.astype(jnp.float32).reshape(1, 1), (4, LANES))
+    info = jnp.concatenate([tail, drop], axis=0)
     dma = pltpu.SemaphoreType.DMA
     held, coherent = pl.pallas_call(
         functools.partial(surfaces, slabs=slabs, groups=groups, own_bins=own_bins, own_w=own_w),
@@ -308,22 +359,25 @@
         out_specs=[pl.BlockSpec(memory_space=pltpu.VMEM)] * 2,
         scratch_shapes=[
             pltpu.VMEM((slabs, groups, 2, local, LANES), jnp.float32),
-            pltpu.VMEM((slabs, 8, LANES), jnp.int32),
+            pltpu.VMEM((slabs, 8, LANES), jnp.float32),
             pltpu.VMEM((2, 8 + BLOCKS * Q // 2, LANES), jnp.float32),
             pltpu.VMEM((own_bins * own_w, 2 * Q), jnp.bfloat16),
             pltpu.VMEM((own_bins * own_w, 2 * Q), jnp.bfloat16),
-            dma((slabs // 2 * groups,)),
-            dma((slabs // 2, groups)),
+            dma((slabs // 4,)),
+            dma((slabs // 4,)),
+            dma((slabs // 4,)),
+            dma((slabs // 4,)),
+            dma((slabs // 4, 2, groups)),
             dma((slabs, groups)),
-            dma((slabs,)),
+            dma((slabs * groups,)),
             dma((slabs,)),
         ],
         compiler_params=pltpu.CompilerParams(
             collective_id=0, has_side_effects=True, vmem_limit_bytes=48 * 2**20
         ),
     )(
-        capture.reshape(2, local, LANES),
-        jnp.broadcast_to(dropped.reshape(1, 1), (8, LANES)),
+        blocks,
+        info,
         ty_hi, ty_lo, tx_hi, tx_lo,
     )
     return held, coherent

time: 52.5 us -> 44.1 us (0.84)
  the two profiles are of different devices: /device:TPU:24 before, /device:TPU:0 now
where the time goes in v3:
time: 44.1 us; the launch traced here: 43.9 us
  Pallas kernels  38.4 us (87%)
  local copies, waits for them, and re-layouts  4.2 us (10%)
  between operations  1.3 us (3%)
    pallas_call x1, Pallas kernels, on_device(): pl.pallas_call(functools.partial(surfaces, slabs=slabs, groups=groups, ow...  38.4 us
    unnamed x7, local copies, waits for them, and re-layouts  2.44 us
    squeeze x1, local copies, waits for them, and re-layouts, on_device(): lax.dynamic_index_in_dim(t, grp, 0, False)  1.05 us

profile of v3, /device:TPU:0, one launch (start us, length us, event | category | flops | bytes accessed | tf_op | source)
XLA Modules:
  0.0 43.9 jit_solution(13113684805439355032)
XLA Ops:
  1.3 0.7 %slice.3 = f32[2,256]{1,0:T(2,128)S(1)} slice(f32[2,8192]{1,0:T(2,128)} %param.6), slice={[0:2], [7936:8192]} | slice | bytes 4096 | tf_op jit(solution)/shard_map/slice | solution.py:348
  2.0 0.8 %copy.10 = f32[1,2,64,128]{3,2,1,0:T(8,128)S(1)} copy(f32[1,2,64,128]{3,1,2,0:T(2,128)} %bitcast.10) | data formatting | bytes 131072
  2.8 0.0 copy-start
  2.8 0.0 copy-start.1
  2.8 1.0 %dynamic-slice_bitcast_fusion = (bf16[128,512]{1,0:T(8,128)(2,1)S(1)}, bf16[128,512]{1,0:T(8,128)(2,1)S(1)}) fusion(bf16[2,128,512]{2,1,0:T(8,128)(2,1)} %constant.23.clone, s32[]{:T(128)S(6)} %select_n.5, bf16[2,128,512]{2,1,0:T(8,128)(2,1)} %constant.22.clone), kind=kLoop, calls=%fused_computation | loop fusion | bytes 524292 | tf_op jit(solution)/shard_map/jit(dynamic_index_in_dim)/squeeze | solution.py:346
  3.9 0.0 copy-done
  3.9 0.1 copy-done.1
  4.0 38.4 %shard_map.77 = (f32[8,64,128]{2,1,0:T(8,128)S(1)}, f32[2,8,64,128]{3,2,1,0:T(8,128)S(1)}) custom-call(f32[2,64,128]{2,1,0:T(8,128)S(1)} %bitcast.9, f32[8,128]{1,0:T(8,128)S(1)} %concatenate.3.own_info, bf16[512,256]{1,0:T(8,128)(2,1)S(1)} %copy-done.1, bf16[512,256]{1,0:T(8,128)(2,1)S(1)} %copy-done, bf16[128,512]{1,0:T(8,128)(2,1)S(1)} %get-tuple-element.3.tx_hi, ...), custom_call_target="tpu_custom_call" | custom-call | tf_op jit(solution)/shard_map/pallas_call | solution.py:352
  42.4 0.7 %copy.14 = f32[8,64,128]{2,1,0:T(8,128)} copy(f32[8,64,128]{2,1,0:T(8,128)S(1)} %get-tuple-element.6) | data formatting | bytes 524288
  43.1 0.8 %copy.15 = f32[2,8,64,128]{3,2,1,0:T(8,128)} copy(f32[2,8,64,128]{3,2,1,0:T(8,128)S(1)} %get-tuple-element.7) | data formatting | bytes 1048576
  (2 shorter events, 0.0 us)
Async XLA Ops:
  2.8 1.1 %copy-start = (bf16[512,256]{1,0:T(8,128)(2,1)S(1)}, bf16[512,256]{1,0:T(8,128)(2,1)}, u32[]{:S(2)}) copy-start(bf16[512,256]{1,0:T(8,128)(2,1)} %constant.21.clone.ty_lo) | copy-start | bytes 786436
  2.8 1.2 %copy-start.1 = (bf16[512,256]{1,0:T(8,128)(2,1)S(1)}, bf16[512,256]{1,0:T(8,128)(2,1)}, u32[]{:S(2)}) copy-start(bf16[512,256]{1,0:T(8,128)(2,1)} %constant.20.clone.ty_hi) | copy-start | bytes 786436

commit v4 on v3

--- a/solution.py
+++ b/solution.py
@@ -72,9 +72,11 @@
 
 def surfaces(
     own_blk, own_info, ty_hi, ty_lo, tx_hi, tx_lo, held, coh,
-    buf, infos, ext, a_hi, a_lo, line_sem, x_sem, y_sem, diag_sem, fwd_sem, recv_sem, isend_sem, irecv_sem,
-    *, slabs, groups, own_bins, own_w
+    buf, infos, ext, *rest,
+    slabs, groups, own_bins, own_w
 ):
+    slots = rest[:4], rest[4:8]
+    line_sem, x_sem, y_sem, diag_sem, fwd_sem, recv_sem, isend_sem, irecv_sem = rest[8:]
     slab, grp = lax.axis_index("slab"), lax.axis_index("grp")
     bits = slabs.bit_length() - 1
     line = slabs // 4
@@ -189,7 +191,6 @@
     zero = slab * 0
     from_x(zero)
     from_y(zero)
-    from_line(zero + 1)
     run(1, slabs, lambda i: info_arrived(flip(slab, i, bits)))
 
     @pl.when(grp != last)
@@ -208,32 +209,29 @@
     def spread(array, count):
         return jnp.concatenate([array[:1]] * count, axis=0)
 
-    def step(t, carry):
+    def events(t):
+        @pl.when((t % 2 == 0) & (t // 2 + 1 < line))
+        def _():
+            from_line(t // 2 + 1)
+
+        @pl.when((t % 2 == 1) & (t >= 3) & (t // 2 < line))
+        def _():
+            from_y(t // 2)
+            from_x(t // 2)
+
+        @pl.when((t % 3 == 2) & (t // 3 < line))
+        def _():
+            from_diagonal(t // 3)
+
+        @pl.when(t % 2 == 1)
+        def _():
+            arrived(t, 0)
+            arrived(t, 1)
+
+    def prepare(t, slot):
         n = flip(slab, t, bits)
         before = (n - 1 + slabs) % slabs
-        kz, part = t // 4, t % 4
-
-        @pl.when((part == 0) & (kz + 2 < line))
-        def _():
-            from_line(kz + 2)
-
-        @pl.when(part == 1)
-        def _():
-            from_diagonal(kz)
-
-        @pl.when((part == 2) & (kz + 1 < line))
-        def _():
-            from_x(kz + 1)
-
-        @pl.when((part == 3) & (kz + 1 < line))
-        def _():
-            from_y(kz + 1)
-
-        @pl.when(part % 2 == 1)
-        def _():
-            arrived(t, 0)
-            arrived(t, 1)
-
+        a_hi, a_lo, w_hi, w_lo = slot
         drops = jnp.zeros((1, LANES), jnp.float32)
         for other in range(slabs):
             drops = drops + infos[other, 4:5, :] * jnp.where(other <= n, 1.0, 0.0)
@@ -286,7 +284,8 @@
                     [jnp.concatenate([zr, -zi], 1), jnp.concatenate([zi, zr], 1)], axis=0
                 )
 
-            y_hi, y_lo = weights(zr_hi, zi_hi), weights(zr_lo, zi_lo)
+            w_hi[b] = weights(zr_hi, zi_hi)
+            w_lo[b] = weights(zr_lo, zi_lo)
             xr = lower[:own_w, b * Q : (b + 1) * Q]
             xi = lower[own_w:, b * Q : (b + 1) * Q]
             ur = xr * phx[0] - xi * phx[1]
@@ -295,17 +294,39 @@
                 c = phq[0][q : q + 1, :]
                 s = phq[1][q : q + 1, :]
                 hi, lo = split(jnp.concatenate([ur * c - ui * s, ur * s + ui * c], axis=1))
-                a_hi[q * own_w : (q + 1) * own_w, :] = hi
-                a_lo[q * own_w : (q + 1) * own_w, :] = lo
-            surf = dot3(a_hi[...], a_lo[...], y_hi, y_lo, ((1,), (0,)))
-            sr = surf[:, :LW].reshape(own_bins, own_w, LW)
-            si = surf[:, LW:].reshape(own_bins, own_w, LW)
-            coh[0] += sr
-            coh[1] += si
-            held[...] = jnp.maximum(held[...], sr * sr + si * si)
+                a_hi[b, q * own_w : (q + 1) * own_w, :] = hi
+                a_lo[b, q * own_w : (q + 1) * own_w, :] = lo
+
+    def accumulate(slot):
+        a_hi, a_lo, w_hi, w_lo = slot
+        surf = [dot3(a_hi[b], a_lo[b], w_hi[b], w_lo[b], ((1,), (0,))) for b in range(BLOCKS)]
+        largest, real, imag = held[...], coh[0], coh[1]
+        for part in surf:
+            sr = part[:, :LW].reshape(own_bins, own_w, LW)
+            si = part[:, LW:].reshape(own_bins, own_w, LW)
+            real, imag = real + sr, imag + si
+            largest = jnp.maximum(largest, sr * sr + si * si)
+        held[...] = largest
+        coh[0] = real
+        coh[1] = imag
+
+    def pair(i, carry):
+        t = 2 * i
+        events(t + 1)
+        prepare(t + 1, slots[1])
+        accumulate(slots[0])
+        events(t + 2)
+        prepare(t + 2, slots[0])
+        accumulate(slots[1])
         return carry
 
-    lax.fori_loop(0, slabs, step, 0)
+    events(zero)
+    prepare(zero, slots[0])
+    lax.fori_loop(0, slabs // 2 - 1, pair, 0)
+    events(zero + slabs - 1)
+    prepare(zero + slabs - 1, slots[1])
+    accumulate(slots[0])
+    accumulate(slots[1])
     held[...] = jnp.sqrt(held[...])
     coh[...] = coh[...] * (1.0 / math.sqrt(slabs * BLOCKS))
 
@@ -349,6 +370,8 @@
     drop = jnp.broadcast_to(dropped.astype(jnp.float32).reshape(1, 1), (4, LANES))
     info = jnp.concatenate([tail, drop], axis=0)
     dma = pltpu.SemaphoreType.DMA
+    slot = [pltpu.VMEM((BLOCKS, own_bins * own_w, 2 * Q), jnp.bfloat16)] * 2
+    slot = slot + [pltpu.VMEM((BLOCKS, 2 * Q, 2 * LW), jnp.bfloat16)] * 2
     held, coherent = pl.pallas_call(
         functools.partial(surfaces, slabs=slabs, groups=groups, own_bins=own_bins, own_w=own_w),
         out_shape=[
@@ -361,8 +384,8 @@
             pltpu.VMEM((slabs, groups, 2, local, LANES), jnp.float32),
             pltpu.VMEM((slabs, 8, LANES), jnp.float32),
             pltpu.VMEM((2, 8 + BLOCKS * Q // 2, LANES), jnp.float32),
-            pltpu.VMEM((own_bins * own_w, 2 * Q), jnp.bfloat16),
-            pltpu.VMEM((own_bins * own_w, 2 * Q), jnp.bfloat16),
+            *slot,
+            *slot,
             dma((slabs // 4,)),
             dma((slabs // 4,)),
             dma((slabs // 4,)),

time: 44.1 us -> 43.5 us (0.986)
  Pallas kernels: 38.4 us -> 37.7 us
    pallas_call x1, Pallas kernels: 38.4 us -> 37.7 us  [on_device(): pl.pallas_call(functools.partial(surfaces, slabs=slabs, groups=groups, ow...]
where the time goes in v4:
time: 43.5 us; the launch traced here: 43.2 us
  Pallas kernels  37.7 us (87%)
  local copies, waits for them, and re-layouts  4.2 us (10%)
  between operations  1.3 us (3%)
    pallas_call x1, Pallas kernels, on_device(): pl.pallas_call(functools.partial(surfaces, slabs=slabs, groups=groups, ow...  37.7 us
    unnamed x7, local copies, waits for them, and re-layouts  2.44 us
    squeeze x1, local copies, waits for them, and re-layouts, on_device(): lax.dynamic_index_in_dim(t, grp, 0, False)  1.05 us

profile of v4, /device:TPU:0, one launch (start us, length us, event | category | flops | bytes accessed | tf_op | source)
XLA Modules:
  0.0 43.2 jit_solution(18326588301311979411)
XLA Ops:
  1.3 0.7 %slice.3 = f32[2,256]{1,0:T(2,128)S(1)} slice(f32[2,8192]{1,0:T(2,128)} %param.6), slice={[0:2], [7936:8192]} | slice | bytes 4096 | tf_op jit(solution)/shard_map/slice | solution.py:369
  2.0 0.8 %copy.10 = f32[1,2,64,128]{3,2,1,0:T(8,128)S(1)} copy(f32[1,2,64,128]{3,1,2,0:T(2,128)} %bitcast.10) | data formatting | bytes 131072
  2.8 0.0 copy-start
  2.8 0.0 copy-start.1
  2.8 1.0 %dynamic-slice_bitcast_fusion = (bf16[128,512]{1,0:T(8,128)(2,1)S(1)}, bf16[128,512]{1,0:T(8,128)(2,1)S(1)}) fusion(bf16[2,128,512]{2,1,0:T(8,128)(2,1)} %constant.23.clone, s32[]{:T(128)S(6)} %select_n.5, bf16[2,128,512]{2,1,0:T(8,128)(2,1)} %constant.22.clone), kind=kLoop, calls=%fused_computation | loop fusion | bytes 524292 | tf_op jit(solution)/shard_map/jit(dynamic_index_in_dim)/squeeze | solution.py:367
  3.9 0.0 copy-done
  3.9 0.1 copy-done.1
  4.0 37.7 %shard_map.77 = (f32[8,64,128]{2,1,0:T(8,128)S(1)}, f32[2,8,64,128]{3,2,1,0:T(8,128)S(1)}) custom-call(f32[2,64,128]{2,1,0:T(8,128)S(1)} %bitcast.9, f32[8,128]{1,0:T(8,128)S(1)} %concatenate.3.own_info, bf16[512,256]{1,0:T(8,128)(2,1)S(1)} %copy-done.1, bf16[512,256]{1,0:T(8,128)(2,1)S(1)} %copy-done, bf16[128,512]{1,0:T(8,128)(2,1)S(1)} %get-tuple-element.3.tx_hi, ...), custom_call_target="tpu_custom_call" | custom-call | tf_op jit(solution)/shard_map/pallas_call | solution.py:375
  41.7 0.7 %copy.14 = f32[8,64,128]{2,1,0:T(8,128)} copy(f32[8,64,128]{2,1,0:T(8,128)S(1)} %get-tuple-element.6) | data formatting | bytes 524288
  42.4 0.8 %copy.15 = f32[2,8,64,128]{3,2,1,0:T(8,128)} copy(f32[2,8,64,128]{3,2,1,0:T(8,128)S(1)} %get-tuple-element.7) | data formatting | bytes 1048576
  (2 shorter events, 0.0 us)
Async XLA Ops:
  2.8 1.1 %copy-start = (bf16[512,256]{1,0:T(8,128)(2,1)S(1)}, bf16[512,256]{1,0:T(8,128)(2,1)}, u32[]{:S(2)}) copy-start(bf16[512,256]{1,0:T(8,128)(2,1)} %constant.21.clone.ty_lo) | copy-start | bytes 786436
  2.8 1.2 %copy-start.1 = (bf16[512,256]{1,0:T(8,128)(2,1)S(1)}, bf16[512,256]{1,0:T(8,128)(2,1)}, u32[]{:S(2)}) copy-start(bf16[512,256]{1,0:T(8,128)(2,1)} %constant.20.clone.ty_hi) | copy-start | bytes 786436
